TPU v7x, 8 devices: a whole 2x2x1 slice. The times are simulated.
8 devices in a mesh: rep: 2 (over y, z), dp: 4 (over x, core).
Axes of the slice: x: 2, y: 2, z: 1, core: 2. Of those that a mesh axis runs over, the one named last changes fastest.
Arguments:
- x: bfloat16 [8, 2048, 768], P(('rep', 'dp')), parts along dimension 0
- dy: bfloat16 [8, 2048, 768], P(('rep', 'dp')), parts along dimension 0
- w_gate: bfloat16 [2, 768, 3072], P(None, 'dp')
- w_up: bfloat16 [2, 768, 3072], P(None, 'dp')
- w_down: bfloat16 [2, 3072, 768], P(None, 'dp')
Outputs:
- output 1: bfloat16 [8, 2048, 768], P(('rep', 'dp')), parts along dimension 0
- output 2: bfloat16 [4, 768, 3072], P('rep', 'dp'), parts along dimension 0
- output 3: bfloat16 [4, 768, 3072], P('rep', 'dp'), parts along dimension 0
- output 4: bfloat16 [4, 3072, 768], P('rep', 'dp'), parts along dimension 0
There are 2 independent parts. A program takes and returns all parts, laid end to end along the dimension named above; an argument that names none is the same for every part.
All inputs are finite; a program needn't handle non-finite values.
Results may differ from a plain program's by a relative error of at most 0.018.
Values are sent between devices in bfloat16 or wider.
A program may use at most 2 GiB of HBM per device.

v0:
```python
import jax
import jax.numpy as jnp
from jax import lax

NAMES = ("w_gate", "w_up", "w_down")


def matmul(a, w):
    return jnp.dot(a, w, preferred_element_type=jnp.float32).astype(jnp.bfloat16)


def normed(h):
    wide = h.astype(jnp.float32)
    scale = lax.rsqrt(jnp.mean(wide**2, -1, keepdims=True) + 1e-6)
    return (wide * scale).astype(jnp.bfloat16)


def layer(h, w):
    a = normed(h)
    gate = jnp.dot(a, w["w_gate"], preferred_element_type=jnp.float32)
    up = jnp.dot(a, w["w_up"], preferred_element_type=jnp.float32)
    return h + matmul((jax.nn.silu(gate) * up).astype(jnp.bfloat16), w["w_down"])


def stack(weights, h):
    for number in range(weights["w_gate"].shape[0]):
        h = layer(h, {name: w[number] for name, w in weights.items()})
    return h


def solution(mesh):
    groups = mesh.shape["rep"]

    def step(x, dy, *weights):
        shape = x.shape
        x, dy = (t.reshape(groups, -1, *t.shape[1:]) for t in (x, dy))

        def of_a_group(x, dy):
            _, back = jax.vjp(stack, dict(zip(NAMES, weights, strict=True)), x)
            by_weights, by_x = back(dy)
            return (by_x, *(by_weights[name] for name in NAMES))

        by_x, *by_weights = jax.vmap(of_a_group)(x, dy)
        return (by_x.reshape(shape), *(t.reshape(-1, *t.shape[2:]) for t in by_weights))

    return step
```

profile of v0, /device:TPU:0, one launch (start us, length us, event | category | flops | bytes accessed | tf_op | source)
XLA Modules:
  0.0 775.4 jit_solution(139949015539841229)
XLA Ops:
  7.2 3.4 fusion.127
  10.6 0.0 all-gather.32.cloned.1.call-start
  10.7 1.6 fusion.126
  12.3 0.0 all-gather.34.cloned.1.call-start
  12.3 3.3 fusion.125
  15.8 0.5 all-gather.36.cloned.1.call-update
  16.3 0.5 all-gather.40.cloned.1.call-update
  16.9 0.5 all-gather.38.cloned.1.call-update
  17.5 0.7 fusion.32
  18.2 2.9 copy.1
  21.1 0.6 multiply_add_fusion.1
  21.7 4.7 copy
  26.4 21.8 %all-gather.30.cloned.1.call-done = bf16[1,768,3072]{2,1,0:T(8,128)(2,1)} async-done(((bf16[1,192,3072]{2,1,0:T(8,128)(2,1)}), bf16[1,768,3072]{2,1,0:T(8,128)(2,1)}) %all-gather.30.cloned.1.call-update) | async-done | bytes 4718608 | tf_op jit(solution)/vmap(jvp())/squeeze | solution.py:27
  48.2 15.9 %fusion.68 = f32[2048,3072]{1,0:T(8,128)} fusion(bf16[1,768,3072]{2,1,0:T(8,128)(2,1)} %all-gather.30.cloned.1.call-done, bf16[1,2048,768]{2,1,0:T(8,128)(2,1)S(1)} %copy-done.4, f32[2048]{0:T(1024)S(1)} %get-tuple-element.13), kind=kOutput, calls=%fused_computation.87 | convolution fusion | flops 9668395008 | bytes 33038336 | tf_op jit(solution)/vmap(jvp())/dot_general | solution.py:20
  64.1 20.7 %all-gather.32.cloned.1.call-done = bf16[1,768,3072]{2,1,0:T(8,128)(2,1)} async-done(((bf16[1,192,3072]{2,1,0:T(8,128)(2,1)}), bf16[1,768,3072]{2,1,0:T(8,128)(2,1)}) %all-gather.32.cloned.1.call-update) | async-done | bytes 4718608 | tf_op jit(solution)/vmap(jvp())/squeeze | solution.py:27
  84.8 15.9 %fusion.64 = f32[2048,3072]{1,0:T(8,128)} fusion(bf16[1,768,3072]{2,1,0:T(8,128)(2,1)} %all-gather.32.cloned.1.call-done, bf16[1,2048,768]{2,1,0:T(8,128)(2,1)S(1)} %copy-done.4, f32[2048]{0:T(1024)S(1)} %get-tuple-element.13), kind=kOutput, calls=%fused_computation.83 | convolution fusion | flops 9668395008 | bytes 33038336 | tf_op jit(solution)/vmap(jvp())/dot_general | solution.py:21
  100.7 21.8 %fusion.24 = bf16[2048,3072]{1,0:T(8,128)(2,1)} fusion(f32[2048,3072]{1,0:T(8,128)} %fusion.64, f32[2048,3072]{1,0:T(8,128)} %fusion.68), kind=kLoop, calls=%fused_computation.34 | loop fusion | flops 37748736 | bytes 62914560
  122.5 16.1 %fusion.40 = (f32[2048]{0:T(1024)S(1)}, bf16[1,1,2048,768]{2,3,1,0:T(8,128)(2,1)}) fusion(bf16[2048,3072]{1,0:T(8,128)(2,1)} %fusion.24, bf16[1,3072,768]{2,1,0:T(8,128)(2,1)} %all-gather.34.cloned.1.call-done, bf16[1,2048,768]{1,2,0:T(8,128)(2,1)S(1)} %copy-done.5), kind=kOutput, calls=%fused_computation.62 | convolution fusion | flops 9671538688 | bytes 23601152 | tf_op jit(solution)/vmap(jvp())/dot_general | solution.py:9
  138.6 18.8 %all-gather.36.cloned.1.call-done = bf16[1,768,3072]{2,1,0:T(8,128)(2,1)} async-done(((bf16[1,192,3072]{2,1,0:T(8,128)(2,1)}), bf16[1,768,3072]{2,1,0:T(8,128)(2,1)}) %all-gather.36.cloned.1.call-update) | async-done | bytes 4718608 | tf_op jit(solution)/vmap(jvp())/squeeze | solution.py:27
  157.5 17.9 %fusion.58 = f32[2048,3072]{1,0:T(8,128)} fusion(bf16[1,768,3072]{2,1,0:T(8,128)(2,1)} %all-gather.36.cloned.1.call-done, bf16[1,1,2048,768]{2,3,1,0:T(8,128)(2,1)} %get-tuple-element.15, f32[2048]{0:T(1024)S(1)} %bitcast.305), kind=kOutput, calls=%fused_computation.77 | convolution fusion | flops 9668395008 | bytes 33038336 | tf_op jit(solution)/vmap(jvp())/dot_general | solution.py:20
  175.3 18.6 %all-gather.40.cloned.1.call-done = bf16[1,768,3072]{2,1,0:T(8,128)(2,1)} async-done(((bf16[1,192,3072]{2,1,0:T(8,128)(2,1)}), bf16[1,768,3072]{2,1,0:T(8,128)(2,1)}) %all-gather.40.cloned.1.call-update) | async-done | bytes 4718608 | tf_op jit(solution)/vmap(jvp())/squeeze | solution.py:27
  194.0 15.8 %fusion.52 = f32[2048,3072]{1,0:T(8,128)} fusion(bf16[1,768,3072]{2,1,0:T(8,128)(2,1)} %all-gather.40.cloned.1.call-done, bf16[1,1,2048,768]{2,3,1,0:T(8,128)(2,1)S(1)} %copy-done.10, f32[2048]{0:T(1024)S(1)} %bitcast.306), kind=kOutput, calls=%fused_computation.71 | convolution fusion | flops 9668395008 | bytes 33038336 | tf_op jit(solution)/vmap(jvp())/dot_general | solution.py:21
  209.7 20.2 %all-gather.38.cloned.1.call-done = bf16[1,3072,768]{2,1,0:T(8,128)(2,1)} async-done(((bf16[1,768,768]{2,1,0:T(8,128)(2,1)}), bf16[1,3072,768]{2,1,0:T(8,128)(2,1)}) %all-gather.38.cloned.1.call-update) | async-done | bytes 4718608 | tf_op jit(solution)/vmap(jvp())/squeeze | solution.py:27
  229.9 13.0 %convolution_convert_fusion.1 = bf16[2048,3072]{1,0:T(8,128)(2,1)S(1)} fusion(bf16[1,3072,768]{2,1,0:T(8,128)(2,1)} %all-gather.38.cloned.1.call-done, bf16[1,2048,768]{2,1,0:T(8,128)(2,1)} %param), kind=kOutput, calls=%fused_computation.42 | convolution fusion | flops 9669967872 | bytes 20447232 | tf_op jit(solution)/vmap(transpose(jvp()))/dot_general | solution.py:9
  242.9 22.9 %fusion.4 = bf16[2048,3072]{1,0:T(8,128)(2,1)S(1)} fusion(f32[2048,3072]{1,0:T(8,128)} %fusion.58, f32[2048,3072]{1,0:T(8,128)} %fusion.52, bf16[2048,3072]{1,0:T(8,128)(2,1)S(1)} %convolution_convert_fusion.1), kind=kLoop, calls=%fused_computation.10 | loop fusion | flops 75497472 | bytes 75497472
  265.8 4.5 copy-done
  270.3 12.8 %fusion.76 = bf16[2048,768]{0,1:T(8,128)(2,1)} fusion(bf16[2048,3072]{1,0:T(8,128)(2,1)S(1)} %fusion.4, bf16[1,768,3072]{2,1,0:T(8,128)(2,1)} %all-gather.36.cloned.1.call-done), kind=kOutput, calls=%fused_computation.91 | convolution fusion | flops 9663676416 | bytes 20447232 | tf_op jit(solution)/vmap(transpose(jvp()))/dot_general | solution.py:20
  283.1 18.0 %fusion.42 = (f32[2048]{0:T(1024)S(1)}, bf16[2048,768]{0,1:T(8,128)(2,1)}) fusion(bf16[1,1,2048,768]{2,3,1,0:T(8,128)(2,1)} %get-tuple-element.15, bf16[2048,768]{0,1:T(8,128)(2,1)} %fusion.76, bf16[1,768,3072]{2,1,0:T(8,128)(2,1)} %all-gather.40.cloned.1.call-done, bf16[2048,3072]{1,0:T(8,128)(2,1)S(1)} %convolution_convert_fusion.1, f32[2048,3072]{1,0:T(8,128)} %fusion.58), kind=kOutput, calls=%fused_computation.64 | convolution fusion | flops 9710860288 | bytes 51912704 | tf_op jit(solution)/vmap(transpose(jvp()))/dot_general | solution.py:21
  301.1 4.2 fusion.93
  305.3 1.6 copy-done.8
  306.9 15.8 %convolution_bitcast_fusion = f32[1,3072,768]{2,1,0:T(8,128)} fusion(bf16[2048,3072]{1,0:T(8,128)(2,1)} %fusion.24, bf16[1,1,2048,768]{2,3,1,0:T(8,128)(2,1)S(1)} %fusion.93), kind=kOutput, calls=%fused_computation.65 | convolution fusion | flops 9663676416 | bytes 25165824 | tf_op jit(solution)/vmap(transpose(jvp()))/dot_general | solution.py:9
  322.7 0.0 reduce-scatter.27.cloned.1.call-start
  322.8 1.8 copy-done.9
  324.6 23.9 %fusion.43 = f32[1,3072,768]{2,1,0:T(8,128)} fusion(f32[2048,3072]{1,0:T(8,128)} %fusion.52, f32[2048,3072]{1,0:T(8,128)} %fusion.58, bf16[1,2048,768]{2,1,0:T(8,128)(2,1)S(1)} %copy-done.9), kind=kOutput, calls=%fused_computation.68 | convolution fusion | flops 9701425152 | bytes 62914560 | tf_op jit(solution)/vmap(transpose(jvp()))/dot_general | solution.py:9
  348.5 0.0 reduce-scatter.23.cloned.1.call-start
  348.6 1.8 copy-done.12
  350.4 19.3 %fusion.46 = f32[1,768,3072]{2,1,0:T(8,128)} fusion(bf16[2048,3072]{1,0:T(8,128)(2,1)} %copy-done.1, f32[2048,3072]{1,0:T(8,128)} %fusion.58, bf16[1,1,2048,768]{2,3,1,0:T(8,128)(2,1)S(1)} %copy-done.12, f32[2048]{0:T(1024)S(1)} %bitcast.308), kind=kOutput, calls=%fused_computation.69 | convolution fusion | flops 9706143744 | bytes 50339840 | tf_op jit(solution)/vmap(transpose(jvp()))/dot_general | solution.py:21
  369.7 0.0 reduce-scatter.25.cloned.1.call-start
  369.7 13.2 %convolution_convert_fusion = bf16[2048,3072]{1,0:T(8,128)(2,1)S(1)} fusion(bf16[1,3072,768]{2,1,0:T(8,128)(2,1)} %all-gather.34.cloned.1.call-done, bf16[1,1,2048,768]{2,3,1,0:T(8,128)(2,1)} %copy-done.8), kind=kOutput, calls=%fused_computation.41 | convolution fusion | flops 9669967872 | bytes 20447232 | tf_op jit(solution)/vmap(transpose(jvp()))/dot_general | solution.py:9
  383.0 22.9 %fusion.7 = bf16[2048,3072]{1,0:T(8,128)(2,1)S(1)} fusion(f32[2048,3072]{1,0:T(8,128)} %fusion.68, f32[2048,3072]{1,0:T(8,128)} %fusion.64, bf16[2048,3072]{1,0:T(8,128)(2,1)S(1)} %convolution_convert_fusion), kind=kLoop, calls=%fused_computation.13 | loop fusion | flops 75497472 | bytes 75497472
  405.9 4.6 copy-done.2
  410.5 12.8 %fusion.70 = bf16[2048,768]{0,1:T(8,128)(2,1)} fusion(bf16[2048,3072]{1,0:T(8,128)(2,1)S(1)} %fusion.7, bf16[1,768,3072]{2,1,0:T(8,128)(2,1)} %all-gather.30.cloned.1.call-done), kind=kOutput, calls=%fused_computation.89 | convolution fusion | flops 9663676416 | bytes 20447232 | tf_op jit(solution)/vmap(transpose(jvp()))/dot_general | solution.py:20
  423.2 18.1 %fusion.38 = (f32[2048]{0:T(1024)S(1)}, bf16[2048,768]{0,1:T(8,128)(2,1)}) fusion(bf16[1,2048,768]{1,2,0:T(8,128)(2,1)} %copy.1, bf16[2048,768]{0,1:T(8,128)(2,1)} %fusion.70, bf16[1,768,3072]{2,1,0:T(8,128)(2,1)} %all-gather.32.cloned.1.call-done, bf16[2048,3072]{1,0:T(8,128)(2,1)S(1)} %convolution_convert_fusion, f32[2048,3072]{1,0:T(8,128)} %fusion.68), kind=kOutput, calls=%fused_computation.60 | convolution fusion | flops 9710860288 | bytes 51912704 | tf_op jit(solution)/vmap(transpose(jvp()))/dot_general | solution.py:21
  441.4 20.0 %fusion.49 = f32[1,768,3072]{2,1,0:T(8,128)} fusion(bf16[2048,3072]{1,0:T(8,128)(2,1)} %copy-done.3, f32[2048,3072]{1,0:T(8,128)} %fusion.68, bf16[1,2048,768]{1,2,0:T(8,128)(2,1)} %copy.1, f32[2048]{0:T(1024)S(1)} %bitcast.310), kind=kOutput, calls=%fused_computation.70 | convolution fusion | flops 9706143744 | bytes 50339840 | tf_op jit(solution)/vmap(transpose(jvp()))/dot_general | solution.py:21
  461.5 1.8 copy-done.13
  463.3 15.0 %convolution_bitcast_fusion.2 = f32[1,768,3072]{2,1,0:T(8,128)} fusion(bf16[2048,3072]{1,0:T(8,128)(2,1)} %copy-done, bf16[1,1,2048,768]{2,3,1,0:T(8,128)(2,1)S(1)} %copy-done.13, f32[2048]{0:T(1024)S(1)} %bitcast.309), kind=kOutput, calls=%fused_computation.67 | convolution fusion | flops 9668395008 | bytes 25174016 | tf_op jit(solution)/vmap(transpose(jvp()))/dot_general | solution.py:20
  478.3 0.0 reduce-scatter.21.cloned.1.call-start
  478.4 1.8 copy-done.6
  480.2 15.2 %convolution_bitcast_fusion.1 = f32[1,768,3072]{2,1,0:T(8,128)} fusion(bf16[2048,3072]{1,0:T(8,128)(2,1)} %copy-done.2, bf16[1,2048,768]{1,2,0:T(8,128)(2,1)S(1)} %copy-done.6, f32[2048]{0:T(1024)S(1)} %bitcast.311), kind=kOutput, calls=%fused_computation.66 | convolution fusion | flops 9668395008 | bytes 25174016 | tf_op jit(solution)/vmap(transpose(jvp()))/dot_general | solution.py:20
  495.5 6.7 fusion.92
  502.2 4.6 copy.2
  506.8 1.8 convert_bitcast_fusion
  508.6 1.8 convert_bitcast_fusion.1
  510.4 1.6 add_bitcast_fusion
  512.0 30.7 %reduce-scatter.23.cloned.1.call-done = f32[1,192,3072]{2,1,0:T(8,128)} async-done(((f32[1,768,3072]{2,1,0:T(8,128)}), f32[1,192,3072]{2,1,0:T(8,128)}) %reduce-scatter.23.cloned.1.call-update) | async-done | bytes 2359312
  542.7 1.8 convert_bitcast_fusion.3
  544.5 72.1 %reduce-scatter.25.cloned.1.call-done = f32[1,192,3072]{2,1,0:T(8,128)} async-done(((f32[1,768,3072]{2,1,0:T(8,128)}), f32[1,192,3072]{2,1,0:T(8,128)}) %reduce-scatter.25.cloned.1.call-update) | async-done | bytes 2359312
  616.6 1.8 convert_bitcast_fusion.2
  618.4 1.6 add_bitcast_fusion.1
  620.0 70.7 %reduce-scatter.19.cloned.1.call-done = f32[1,192,3072]{2,1,0:T(8,128)} async-done(((f32[1,768,3072]{2,1,0:T(8,128)}), f32[1,192,3072]{2,1,0:T(8,128)}) %reduce-scatter.19.cloned.1.call-update) | async-done | bytes 2359312
  690.8 1.8 convert_bitcast_fusion.5
  692.6 72.1 %reduce-scatter.21.cloned.1.call-done = f32[1,192,3072]{2,1,0:T(8,128)} async-done(((f32[1,768,3072]{2,1,0:T(8,128)}), f32[1,192,3072]{2,1,0:T(8,128)}) %reduce-scatter.21.cloned.1.call-update) | async-done | bytes 2359312
  764.7 1.8 convert_bitcast_fusion.4
  766.5 1.6 add_bitcast_fusion.2
  (51 shorter events, 0.5 us)
Async XLA Ops:
  7.2 3.5 copy-start.14
  7.2 41.0 %all-gather.30.cloned.1.call-start = ((), (), s32[]{:S(2)}) async-start(), calls=%async_computation.6 | async-start | bytes 5898240 | tf_op jit(solution)/vmap(jvp())/squeeze | solution.py:27
  10.6 74.2 %all-gather.32.cloned.1.call-start = ((), (), s32[]{:S(2)}) async-start(), calls=%async_computation.7 | async-start | bytes 5898240 | tf_op jit(solution)/vmap(jvp())/squeeze | solution.py:27
  12.3 5.2 copy-start.4
  12.3 110.2 %all-gather.34.cloned.1.call-start = ((), (), s32[]{:S(2)}) async-start(), calls=%async_computation.8 | async-start | bytes 5898240 | tf_op jit(solution)/vmap(jvp())/squeeze | solution.py:27
  15.7 141.7 %all-gather.36.cloned.1.call-start = ((), (), s32[]{:S(2)}) async-start(), calls=%async_computation.9 | async-start | bytes 5898240 | tf_op jit(solution)/vmap(jvp())/squeeze | solution.py:27
  16.3 177.7 %all-gather.40.cloned.1.call-start = ((), (), s32[]{:S(2)}) async-start(), calls=%async_computation.11 | async-start | bytes 5898240 | tf_op jit(solution)/vmap(jvp())/squeeze | solution.py:27
  16.9 213.0 %all-gather.38.cloned.1.call-start = ((), (), s32[]{:S(2)}) async-start(), calls=%async_computation.10 | async-start | bytes 5898240 | tf_op jit(solution)/vmap(jvp())/squeeze | solution.py:27
  17.4 489.4 %reduce-scatter.29.cloned.1.call-start = ((), (), s32[]{:S(2)}) async-start(), calls=%async_computation.17 | async-start | bytes 11796480
  100.7 21.8 %copy-start.5 = (bf16[1,2048,768]{1,2,0:T(8,128)(2,1)S(1)}, bf16[1,2048,768]{1,2,0:T(8,128)(2,1)}, u32[]{:S(2)}) copy-start(bf16[1,2048,768]{1,2,0:T(8,128)(2,1)} %copy.1) | copy-start | bytes 9437188
  138.6 210.0 %copy-start.15 = (f32[1,1,2048]{2,1,0:T(1,128)}, f32[1,1,2048]{2,1,0:T(1,128)S(1)}, u32[]{:S(2)}) copy-start(f32[1,1,2048]{2,1,0:T(1,128)S(1)} %rsqrt.23) | copy-start | bytes 24580
  157.4 36.5 %copy-start.10 = (bf16[1,1,2048,768]{2,3,1,0:T(8,128)(2,1)S(1)}, bf16[1,1,2048,768]{2,3,1,0:T(8,128)(2,1)}, u32[]{:S(2)}) copy-start(bf16[1,1,2048,768]{2,3,1,0:T(8,128)(2,1)} %get-tuple-element.15) | copy-start | bytes 9437188
  242.9 40.2 %copy-start.1 = (bf16[2048,3072]{1,0:T(8,128)(2,1)}, bf16[2048,3072]{1,0:T(8,128)(2,1)S(1)}, u32[]{:S(2)}) copy-start(bf16[2048,3072]{1,0:T(8,128)(2,1)S(1)} %convolution_convert_fusion.1) | copy-start | bytes 37748740
  265.8 4.5 copy-start
  283.1 18.0 %copy-start.7 = (bf16[1,2048,768]{1,2,0:T(8,128)(2,1)S(1)}, bf16[1,2048,768]{1,2,0:T(8,128)(2,1)}, u32[]{:S(2)}) copy-start(bf16[1,2048,768]{1,2,0:T(8,128)(2,1)} %copy) | copy-start | bytes 9437188
  283.1 18.0 %copy-start.11 = (bf16[1,1,2048,768]{2,3,1,0:T(8,128)(2,1)S(1)}, bf16[1,1,2048,768]{2,3,1,0:T(8,128)(2,1)}, u32[]{:S(2)}) copy-start(bf16[1,1,2048,768]{2,3,1,0:T(8,128)(2,1)} %get-tuple-element.15) | copy-start | bytes 9437188
  305.3 1.6 copy-start.8
  322.7 1.9 copy-start.9
  322.7 185.9 %reduce-scatter.27.cloned.1.call-start = ((), (), s32[]{:S(2)}) async-start(), calls=%async_computation.16 | async-start | bytes 11796480
  348.5 1.9 copy-start.12
  348.5 194.1 %reduce-scatter.23.cloned.1.call-start = ((), (), s32[]{:S(2)}) async-start(), calls=%async_computation.14 | async-start | bytes 11796480
  369.7 246.9 %reduce-scatter.25.cloned.1.call-start = ((), (), s32[]{:S(2)}) async-start(), calls=%async_computation.15 | async-start | bytes 11796480
  383.0 40.2 %copy-start.3 = (bf16[2048,3072]{1,0:T(8,128)(2,1)}, bf16[2048,3072]{1,0:T(8,128)(2,1)S(1)}, u32[]{:S(2)}) copy-start(bf16[2048,3072]{1,0:T(8,128)(2,1)S(1)} %convolution_convert_fusion) | copy-start | bytes 37748740
  405.9 4.6 copy-start.2
  423.2 18.1 %copy-start.17 = (f32[2048]{0:T(1024)S(1)}, f32[2048]{0:T(1024)}, u32[]{:S(2)}) copy-start(f32[2048]{0:T(1024)} %get-tuple-element.12) | copy-start | bytes 24580
  461.4 1.9 copy-start.13
  461.4 1.9 copy-start.16
  461.4 229.3 %reduce-scatter.19.cloned.1.call-start = ((), (), s32[]{:S(2)}) async-start(), calls=%async_computation.12 | async-start | bytes 11796480
  478.3 1.9 copy-start.6
  478.3 286.4 %reduce-scatter.21.cloned.1.call-start = ((), (), s32[]{:S(2)}) async-start(), calls=%async_computation.13 | async-start | bytes 11796480
Sparse Core Ops, SparseCore 0:
  10.8 37.3 all-gather.29
  50.3 34.5 all-gather.31
  86.4 34.5 all-gather.33
  122.9 34.5 all-gather.35
  159.4 34.5 all-gather.39
  195.3 34.5 all-gather.37
  322.9 71.5 reduce-scatter.28
  397.0 71.5 reduce-scatter.26
  471.1 71.5 reduce-scatter.22
  545.1 71.5 reduce-scatter.24
  619.2 71.5 reduce-scatter.18
  693.2 71.5 reduce-scatter.20
where the time goes:
time: 785 us; the launch traced here: 775 us
  waiting for transfers between devices  348 us (44%)
  matrix products  279 us (36%)
  other arithmetic  95.2 us (12%)
  local copies, waits for them, and re-layouts  38.6 us (5%)
  between operations  14.9 us (2%)
    unnamed x18, waiting for transfers between devices  247 us
    dot_general x6, matrix products, layer(): up = jnp.dot(a, w['w_up'], preferred_element_type=jnp.float32)  107 us
    squeeze x6, waiting for transfers between devices, stack(): h = layer(h, {name: w[number] for name, w in weights.items()})  100 us
    dot_general x6, matrix products, layer(): gate = jnp.dot(a, w['w_gate'], preferred_element_type=jnp.float32)  89.6 us
    dot_general x5, matrix products, matmul(): jnp.dot(a, w, preferred_element_type=jnp.float32).astype(jnp.bfloat16)  82 us
    unnamed x3, other arithmetic  67.5 us
    unnamed x39, local copies, waits for them, and re-layouts  30.2 us
  transfers between devices with their start and end apart: 12, of which 9 were waited for; matrix products, arithmetic and copies ran while one was open for 39% of the time, Pallas kernels for 0%

commit v1 on v0

v1 whole, which is shorter than its diff:
```python
import functools

import jax
import jax.numpy as jnp
from jax import lax
from jax.experimental import pallas as pl
from jax.experimental.pallas import tpu as pltpu
from jax.sharding import PartitionSpec as P

BF, F32 = jnp.bfloat16, jnp.float32
MESH = pl.DeviceIdType.MESH
TB = 512


def pos(q):
    return (q % 2) * 2 + q // 2


def dot(a, b):
    return jnp.dot(a, b, preferred_element_type=F32)


def dot_t(a, b):
    return lax.dot_general(a, b, (((1,), (1,)), ((), ())), preferred_element_type=F32)


def kernel(NC, x_h, dy_h, wg_h, wu_h, wd_h,
           dx_o, og_o, ou_o, od_o, gxg, gxu, gxd, gdg, gdu, gdd, psg, psu, psd,
           hb, dyb, ab, aT, acc, WG, WU, WD, pT, dgb, dub,
           szg, szu, szd, rzg, rzu, rzd, Gg, Gu, Gd, sxg, sxu, sxd, rxg, rxu, rxd, obg, obu, obd,
           io_s, ld_s, ps_s, ps_r, ax_s, ax_r, ay_s, ay_r, az_s, az_r,
           z_s, z_r, x_s, x_r, o_s):
    T, D = ab.shape
    FC = dgb.shape[1]
    L = wg_h.shape[0]
    Q = wg_h.shape[1]
    S = FC // 4
    FD = wd_h.shape[1]
    Q2, S2 = Q // 2, S // 2
    NB = T // TB
    r = lax.axis_index("rep")
    me = lax.axis_index("dp")
    c, k = me // 2, me % 2
    xp = {"rep": r, "dp": (1 - c) * 2 + k}
    yp = {"rep": 1 - r, "dp": me}
    zp = {"rep": r, "dp": c * 2 + 1 - k}
    zq = c * 2 + 1 - k
    xq = (1 - c) * 2 + k
    dq = (1 - c) * 2 + 1 - k

    def m_of(i, n):
        return pl.multiple_of(i, n)

    def remote(src, dst, ss, rs, dev):
        return pltpu.make_async_remote_copy(src, dst, ss, rs, device_id=dev, device_id_type=MESH)

    def half(m, h):
        n = S2 if m == 2 else Q2
        return pl.ds(m_of(h * n, n), n)

    W_in = (wg_h, wu_h, wd_h)
    GX, GD, PS, WV = (gxg, gxu, gxd), (gdg, gdu, gdd), (psg, psu, psd), (WG, WU, WD)

    def strips(m, l, j, h=None):
        if m == 2:
            n = S if h is None else S2
            at = j * S if h is None else j * S + h * S2
            return [((l, pl.ds(m_of(at, n), n), slice(None)), None)]
        rows = slice(None) if h is None else half(m, h)
        return [((l, rows, pl.ds(m_of(d * FD + j * S, S), S)), pl.ds(pos(d) * S, S)) for d in range(4)]

    def send_x(s):
        l, j = s // NC, s % NC
        for m in range(3):
            for src, cols in strips(m, l, j, r):
                dst = GX[m].at[l, j, half(m, r)] if cols is None else GX[m].at[l, j, half(m, r), cols]
                remote(W_in[m].at[src], dst, ax_s.at[m, s], ax_r.at[m, s], xp).start()

    def send_ps(l):
        for m in range(3):
            remote(W_in[m].at[l], PS[m].at[l], ps_s.at[m, l], ps_r.at[m, l], zp).start()

    def whole(m, s, h, ss, rs, dev, G=None):
        l, j = s // NC, s % NC
        src = GX[m].at[l, j, half(m, h)]
        return remote(src, (G or GX)[m].at[l, j, half(m, h)], ss, rs, dev)

    def stage1(s):
        for m in range(3):
            whole(m, s, r, ax_s.at[m, s], ax_r.at[m, s], xp).wait_recv()
            whole(m, s, r, ay_s.at[m, s], ay_r.at[m, s], yp).start()
            whole(m, s, r, az_s.at[0, m, s], az_r.at[0, m, s], zp, GD).start()

    def stage2(s):
        for m in range(3):
            whole(m, s, 1 - r, ay_s.at[m, s], ay_r.at[m, s], yp).wait_recv()
            whole(m, s, 1 - r, az_s.at[1, m, s], az_r.at[1, m, s], zp, GD).start()

    def ready(s):
        for i in range(2):
            for m in range(3):
                whole(m, s, r if i == 0 else 1 - r, az_s.at[i, m, s], az_r.at[i, m, s], zp, GD).wait_recv()

        @pl.when(s % NC == 0)
        def _():
            l = s // NC
            for m in range(3):
                remote(W_in[m].at[l], PS[m].at[l], ps_s.at[m, l], ps_r.at[m, l], zp).wait_recv()

    def drain_ag():
        @pl.loop(0, L * NC)
        def _(s):
            for m in range(3):
                whole(m, s, r, ax_s.at[m, s], ax_r.at[m, s], xp).wait_send()
                whole(m, s, r, ay_s.at[m, s], ay_r.at[m, s], yp).wait_send()
                for i in range(2):
                    whole(m, s, r, az_s.at[i, m, s], az_r.at[i, m, s], zp, GD).wait_send()
        for l in range(L):
            for m in range(3):
                remote(W_in[m].at[l], PS[m].at[l], ps_s.at[m, l], ps_r.at[m, l], zp).wait_send()

    def load(step):
        l, j, slot = (step // NC) % 2, step % NC, step % 2
        for m in range(3):
            for q, src in ((me, W_in[m]), (zq, PS[m])):
                for at, cols in strips(m, l, j):
                    if m == 2:
                        dst = WV[m].at[slot, pl.ds(m_of(((q % 2) * 2 + q // 2) * S, S), S)]
                    else:
                        dst = WV[m].at[slot, pl.ds(m_of(q * Q, Q), Q), cols]
                    pltpu.make_async_copy(src.at[at], dst, ld_s.at[m, slot]).start()
            for q, src in ((xq, GX[m]), (dq, GD[m])):
                if m == 2:
                    dst = WV[m].at[slot, pl.ds(m_of(((q % 2) * 2 + q // 2) * S, S), S)]
                else:
                    dst = WV[m].at[slot, pl.ds(m_of(q * Q, Q), Q)]
                pltpu.make_async_copy(src.at[l, j], dst, ld_s.at[m, slot]).start()

    def loaded(step):
        slot = step % 2
        for m in range(3):
            pltpu.make_async_copy(WV[m].at[slot], WV[m].at[slot], ld_s.at[m, slot]).wait()

    SZ, RZ, G32, SX, RX, OB = (szg, szu, szd), (rzg, rzu, rzd), (Gg, Gu, Gd), (sxg, sxu, sxd), (rxg, rxu, rxd), (obg, obu, obd)
    HR = (2 * Q, 2 * Q, 2 * S)
    QR = (Q, Q, S)

    def to_z(m, s):
        return remote(SZ[m], RZ[m].at[s % 2], z_s.at[m], z_r.at[m, s % 2], zp)

    def to_x(m, s):
        return remote(SX[m].at[s % 2], RX[m].at[s % 4], x_s.at[m, s % 2], x_r.at[m, s % 4], xp)

    def grads(s, base, m):
        rows = pl.ds(m_of(base * HR[m], HR[m]), HR[m])
        if m == 2:
            return dot(pT[rows, :], dyb[...])
        return dot(aT[rows, :], (dgb, dub)[m][...])

    def produce(s):
        for m in (2, 0, 1):
            SZ[m][...] = grads(s, 1 - k, m).astype(BF)
            to_z(m, s).start()
        for m in (2, 0, 1):
            G32[m][s % 2] = grads(s, k, m)

    def reduce_x(s):
        for m in (2, 0, 1):
            @pl.when(s >= 2)
            def _():
                to_x(m, s).wait_send()
            to_z(m, s).wait()
            mine, other = pl.ds(m_of(c * QR[m], QR[m]), QR[m]), pl.ds(m_of((1 - c) * QR[m], QR[m]), QR[m])
            SX[m][s % 2] = (G32[m][s % 2, other] + RZ[m][s % 2, other].astype(F32)).astype(BF)
            to_x(m, s).start()
            G32[m][s % 2, mine] += RZ[m][s % 2, mine].astype(F32)

    def out_copies(s):
        l, j = 1 - s // NC, s % NC
        for m in range(3):
            for at, cols in strips(m, l, j):
                src = OB[m].at[s % 2] if cols is None else OB[m].at[s % 2, :, cols]
                yield pltpu.make_async_copy(src, (og_o, ou_o, od_o)[m].at[at], o_s.at[m, s % 2])

    def out_wait(s):
        for m in range(3):
            pltpu.make_async_copy(OB[m].at[s % 2], OB[m].at[s % 2], o_s.at[m, s % 2]).wait()

    def finish(s):
        @pl.when(s >= 2)
        def _():
            out_wait(s)
        for m in (2, 0, 1):
            to_x(m, s).wait_recv()
            mine = pl.ds(m_of(c * QR[m], QR[m]), QR[m])
            OB[m][s % 2] = (G32[m][s % 2, mine] + RX[m][s % 4].astype(F32)).astype(BF)
        for copy in out_copies(s):
            copy.start()

    def scale_of(wide):
        return lax.rsqrt(jnp.mean(wide * wide, -1, keepdims=True) + 1e-6)

    def norm(l, transposed):
        @pl.loop(0, T // 256)
        def _(t):
            rows = pl.ds(m_of(t * 256, 256), 256)
            wide = hb[l, rows, :].astype(F32)
            a = (wide * scale_of(wide)).astype(BF)
            ab[rows, :] = a
            acc[rows, :] = jnp.zeros((256, D), F32)
            if transposed:
                at = a.T
                for q in range(4):
                    aT[pl.ds(pos(q) * Q, Q), rows] = at[q * Q:(q + 1) * Q]

    def fwd_block(slot, t):
        rows = pl.ds(m_of(t * TB, TB), TB)
        a = ab[rows, :]
        ps = []
        for n in range(0, FC, 256):
            g = dot(a, WG[slot, :, n:n + 256])
            u = dot(a, WU[slot, :, n:n + 256])
            p = (g * (1.0 / (1.0 + jnp.exp(-g))) * u).astype(BF)
            ps.append(p)
        acc[rows, :] += dot(jnp.concatenate(ps, 1), WD[slot])

    def bwd_block(slot, t):
        rows = pl.ds(m_of(t * TB, TB), TB)
        a = ab[rows, :]
        dy = dyb[rows, :]
        for n in range(0, FC, 256):
            g = dot(a, WG[slot, :, n:n + 256])
            u = dot(a, WU[slot, :, n:n + 256])
            dp = dot_t(dy, WD[slot, n:n + 256, :]).astype(BF).astype(F32)
            sig = 1.0 / (1.0 + jnp.exp(-g))
            silu = g * sig
            p = (silu * u).astype(BF)
            pT[n:n + 256, rows] = p.T
            dub[rows, n:n + 256] = (dp * silu).astype(BF)
            dgb[rows, n:n + 256] = (dp * u * (sig * (1.0 + g * (1.0 - sig)))).astype(BF)
        acc[rows, :] += dot_t(dgb[rows, :], WG[slot]) + dot_t(dub[rows, :], WU[slot])

    def norm_back(l):
        @pl.loop(0, T // 256)
        def _(t):
            rows = pl.ds(m_of(t * 256, 256), 256)
            wide = hb[l, rows, :].astype(F32)
            sc = scale_of(wide)
            da = acc[rows, :].astype(BF).astype(F32)
            inner = jnp.sum(da * wide, -1, keepdims=True)
            dh = da * sc - wide * (sc * sc * sc * inner * (1.0 / D))
            dyb[rows, :] = (dyb[rows, :].astype(F32) + dh.astype(BF).astype(F32)).astype(BF)

    in_x = pltpu.make_async_copy(x_h, hb.at[0], io_s.at[0])
    in_dy = pltpu.make_async_copy(dy_h, dyb, io_s.at[1])
    in_x.start()
    in_dy.start()
    barrier = pltpu.get_barrier_semaphore()
    for dev in (xp, yp, zp):
        pl.semaphore_signal(barrier, inc=1, device_id=dev, device_id_type=MESH)
    pl.semaphore_wait(barrier, 3)
    send_x(0)
    send_ps(0)

    @pl.loop(1, NC)
    def _(s):
        send_x(s)
    in_x.wait()
    norm(0, False)
    in_dy.wait()
    stage1(0)
    stage1(1)
    stage2(0)
    ready(0)
    load(0)

    @pl.loop(0, NC)
    def _(j):
        loaded(j)
        send_x(NC + j)

        @pl.when(j == 0)
        def _():
            send_ps(1)

        @pl.loop(0, NB)
        def _(t):
            fwd_block(j % 2, t)

            @pl.when(t == 0)
            def _():
                stage1(j + 2)

            @pl.when(t == 1)
            def _():
                stage2(j + 1)

            @pl.when(t == 2)
            def _():
                ready(j + 1)
                load(j + 1)

    @pl.loop(0, T // 256)
    def _(t):
        rows = pl.ds(m_of(t * 256, 256), 256)
        hb[1, rows, :] = (hb[0, rows, :].astype(F32) + acc[rows, :].astype(BF).astype(F32)).astype(BF)

    @pl.loop(0, 2)
    def _(phase):
        norm(1 - phase, True)

        @pl.loop(0, NC)
        def _(j):
            s = phase * NC + j
            step = NC + s
            loaded(step)

            @pl.loop(0, NB)
            def _(t):
                bwd_block(step % 2, t)

                @pl.when(t == 0)
                def _():
                    @pl.when(s >= 1)
                    def _():
                        reduce_x(s - 1)

                    @pl.when(step + 2 < 2 * NC)
                    def _():
                        stage1(step + 2)

                @pl.when(t == 1)
                def _():
                    @pl.when(step + 1 < 2 * NC)
                    def _():
                        stage2(step + 1)

                @pl.when(t == 2)
                def _():
                    @pl.when(s >= 2)
                    def _():
                        finish(s - 2)

                    @pl.when(step + 1 < 2 * NC)
                    def _():
                        ready(step + 1)

                    @pl.when(step + 1 < 3 * NC)
                    def _():
                        load(step + 1)
            produce(s)
        norm_back(1 - phase)

    last = 2 * NC - 1
    out_dx = pltpu.make_async_copy(dyb, dx_o, io_s.at[0])
    out_dx.start()
    reduce_x(last)
    finish(last - 1)
    drain_ag()
    finish(last)
    for s in (last - 1, last):
        for m in range(3):
            to_x(m, s).wait_send()
        out_wait(s)
    out_dx.wait()


def solution(mesh):
    def local(x, dy, wg, wu, wd):
        _, T, D = x.shape
        L, Q, F = wg.shape
        FD = wd.shape[1]
        NC = 6
        FC = F // NC
        S = FC // 4
        sds = jax.ShapeDtypeStruct
        hbm = pl.BlockSpec(memory_space=pltpu.HBM)
        V, DMA = pltpu.VMEM, pltpu.SemaphoreType.DMA
        gate, down = (L, NC, Q, FC), (L, NC, S, D)
        outs = [sds((T, D), BF), sds(wg.shape, BF), sds(wu.shape, BF), sds(wd.shape, BF)]
        outs += [sds(s, BF) for s in (gate, gate, down) * 2]
        outs += [sds(t.shape, BF) for t in (wg, wu, wd)]
        scratch = [V((2, T, D), BF), V((T, D), BF), V((T, D), BF), V((D, T), BF), V((T, D), F32),
                   V((2, D, FC), BF), V((2, D, FC), BF), V((2, FC, D), BF),
                   V((FC, T), BF), V((T, FC), BF), V((T, FC), BF)]
        h3 = ((2 * Q, FC), (2 * Q, FC), (2 * S, D))
        q3 = ((Q, FC), (Q, FC), (S, D))
        scratch += [V(s, BF) for s in h3] + [V((2, *s), BF) for s in h3] + [V((2, *s), F32) for s in h3]
        scratch += [V((2, *s), BF) for s in q3] + [V((4, *s), BF) for s in q3] + [V((2, *s), BF) for s in q3]
        LC = L * NC
        scratch += [DMA((2,)), DMA((3, 2)), DMA((3, L)), DMA((3, L)), DMA((3, LC)), DMA((3, LC)), DMA((3, LC)), DMA((3, LC)),
                    DMA((2, 3, LC)), DMA((2, 3, LC)), DMA((3,)), DMA((3, 2)), DMA((3, 2)), DMA((3, 4)), DMA((3, 2))]
        res = pl.pallas_call(
            functools.partial(kernel, NC),
            out_shape=outs,
            in_specs=[hbm] * 5,
            out_specs=[hbm] * len(outs),
            scratch_shapes=scratch,
            compiler_params=pltpu.CompilerParams(collective_id=0, has_side_effects=True, vmem_limit_bytes=67043328),
        )(x[0], dy[0], wg, wu, wd)
        return (res[0][None], *res[1:4])

    seq, w = P(("rep", "dp"), None, None), P(None, "dp", None)
    grad = P("rep", "dp", None)
    return jax.shard_map(local, mesh=mesh, in_specs=(seq, seq, w, w, w), out_specs=(seq, grad, grad, grad), check_vma=False)
```

time: 785 us -> 314 us (0.40); the launches traced: 775 us -> 314 us
  waiting for transfers between devices: 348 us -> 0 us
  Pallas kernels: 0 us -> 303 us
  matrix products: 279 us -> 0 us
  other arithmetic: 95.2 us -> 0 us
  local copies, waits for them, and re-layouts: 38.6 us -> 10.3 us
  between operations: 14.9 us -> 0.65 us
    pallas_call x0 -> x1, Pallas kernels: none -> 303 us  [local(): pl.pallas_call(functools.partial(kernel, NC), out_shape=outs, in_specs=[h...]
    dot_general x17 -> x0, matrix products: 279 us -> none  [the longest x6 107 us: layer(): up = jnp.dot(a, w['w_up'], preferred_element_type=jnp.float32)]
    unnamed x18 -> x0, waiting for transfers between devices: 247 us -> none
    squeeze x6 -> x0, waiting for transfers between devices: 100 us -> none  [stack(): h = layer(h, {name: w[number] for name, w in weights.items()})]
    unnamed x3 -> x0, other arithmetic: 67.5 us -> none
    unnamed x39 -> x10, local copies, waits for them, and re-layouts: 30.2 us -> 10.3 us
    reshape x4 -> x0, other arithmetic: 11.4 us -> none  [the longest x1 6.71 us: step(): by_x.reshape(shape)]
    broadcast_in_dim x6 -> x0, other arithmetic: 10.8 us -> none  [stack(): h = layer(h, {name: w[number] for name, w in weights.items()})]
  transfers between devices with their start and end apart: 12 -> 0, of which waited for: 9 -> 0; matrix products, arithmetic and copies ran while one was open for 39% -> 0% of each run, Pallas kernels for 0% -> 0%
where the time goes in v1:
time: 314 us
  Pallas kernels  303 us (96%)
  local copies, waits for them, and re-layouts  10.3 us (3%)
    pallas_call x1, Pallas kernels, local(): pl.pallas_call(functools.partial(kernel, NC), out_shape=outs, in_specs=[h...  303 us
    unnamed x10, local copies, waits for them, and re-layouts  10.3 us

profile of v1, /device:TPU:0, one launch (start us, length us, event | category | flops | bytes accessed | tf_op | source)
XLA Modules:
  0.0 313.9 jit_solution(17564466032299492312)
XLA Ops:
  0.6 302.9 %shard_map.84 = (bf16[2048,768]{1,0:T(8,128)(2,1)}, bf16[2,192,3072]{2,1,0:T(8,128)(2,1)}, bf16[2,192,3072]{2,1,0:T(8,128)(2,1)}, bf16[2,768,768]{2,1,0:T(8,128)...) custom-call(bf16[2048,768]{1,0:T(8,128)(2,1)} %bitcast.4, ...), custom_call_target="tpu_custom_call" | custom-call | tf_op jit(solution)/shard_map/pallas_call | solution.py:393
  303.5 0.0 copy-start.2
  303.5 3.9 %copy.13 = bf16[1,2048,768]{2,1,0:T(8,128)(2,1)} copy(bf16[1,2048,768]{2,1,0:T(8,128)(2,1)} %bitcast.3) | data formatting | bytes 6291456
  307.4 0.0 copy-done.2
  307.4 0.0 copy-start.1
  307.4 1.4 copy.14
  308.8 1.1 copy-done.1
  309.9 0.0 copy-start
  309.9 1.4 copy.15
  311.3 1.1 copy-done
  312.5 1.4 copy.16
Async XLA Ops:
  303.5 3.9 %copy-start.2 = (bf16[2,192,3072]{2,1,0:T(8,128)(2,1)S(1)}, bf16[2,192,3072]{2,1,0:T(8,128)(2,1)}, u32[]{:S(2)}) copy-start(bf16[2,192,3072]{2,1,0:T(8,128)(2,1)} %get-tuple-element.17) | copy-start | bytes 7077892
  307.4 2.5 copy-start.1
  309.9 2.5 copy-start

commit v2 on v1

--- a/solution.py
+++ b/solution.py
@@ -25,8 +25,8 @@
 
 
 def kernel(NC, x_h, dy_h, wg_h, wu_h, wd_h,
-           dx_o, og_o, ou_o, od_o, gxg, gxu, gxd, gdg, gdu, gdd, psg, psu, psd,
-           hb, dyb, ab, aT, acc, WG, WU, WD, pT, dgb, dub,
+           dx_o, og_o, ou_o, od_o, gxg, gxu, gxd, gdg, gdu, gdd, psg, psu, psd, g_h, u_h,
+           hb, dyb, ab, aT, acc, WG, WU, WD, pT, dgb, dub, gst, ust, gu_s,
            szg, szu, szd, rzg, rzu, rzd, Gg, Gu, Gd, sxg, sxu, sxd, rxg, rxu, rxd, obg, obu, obd,
            io_s, ld_s, ps_s, ps_r, ax_s, ax_r, ay_s, ay_r, az_s, az_r,
            z_s, z_r, x_s, x_r, o_s):
@@ -151,18 +151,25 @@
     def to_x(m, s):
         return remote(SX[m].at[s % 2], RX[m].at[s % 4], x_s.at[m, s % 2], x_r.at[m, s % 4], xp)
 
-    def grads(s, base, m):
-        rows = pl.ds(m_of(base * HR[m], HR[m]), HR[m])
+    def grads(m, part, n):
+        rows = pl.ds(m_of(part * HR[m], HR[m]), HR[m])
         if m == 2:
-            return dot(pT[rows, :], dyb[...])
-        return dot(aT[rows, :], (dgb, dub)[m][...])
+            return dot(pT[rows, :], dyb[:, n:n + 256])
+        return dot(aT[rows, :], (dgb, dub)[m][:, n:n + 256])
 
     def produce(s):
+        slot = s % 2
+        for n in range(0, D, 256):
+            szd[:, n:n + 256] = grads(2, 1 - k, n).astype(BF)
+            Gd[slot, :, n:n + 256] = grads(2, k, n)
+        for m in (0, 1):
+            for n in range(0, FC, 256):
+                SZ[m][:, n:n + 256] = grads(m, 1 - k, n).astype(BF)
         for m in (2, 0, 1):
-            SZ[m][...] = grads(s, 1 - k, m).astype(BF)
             to_z(m, s).start()
-        for m in (2, 0, 1):
-            G32[m][s % 2] = grads(s, k, m)
+        for m in (0, 1):
+            for n in range(0, FC, 256):
+                G32[m][slot, :, n:n + 256] = grads(m, k, n)
 
     def reduce_x(s):
         for m in (2, 0, 1):
@@ -213,32 +220,49 @@
                 for q in range(4):
                     aT[pl.ds(pos(q) * Q, Q), rows] = at[q * Q:(q + 1) * Q]
 
-    def fwd_block(slot, t):
+    def gu_copies(j, t, out):
         rows = pl.ds(m_of(t * TB, TB), TB)
+        for i, (v, h) in enumerate(((gst, g_h), (ust, u_h))):
+            pair = (v.at[t % 2], h.at[j, rows, :])
+            yield pltpu.make_async_copy(*(pair if out else pair[::-1]), gu_s.at[i, t % 2])
+
+    def fwd_block(slot, j, t):
+        rows = pl.ds(t * TB, TB)
         a = ab[rows, :]
         ps = []
         for n in range(0, FC, 256):
             g = dot(a, WG[slot, :, n:n + 256])
             u = dot(a, WU[slot, :, n:n + 256])
-            p = (g * (1.0 / (1.0 + jnp.exp(-g))) * u).astype(BF)
-            ps.append(p)
-        acc[rows, :] += dot(jnp.concatenate(ps, 1), WD[slot])
-
-    def bwd_block(slot, t):
-        rows = pl.ds(m_of(t * TB, TB), TB)
-        a = ab[rows, :]
+            gst[t % 2, :, n:n + 256] = g
+            ust[t % 2, :, n:n + 256] = u
+            ps.append((g * (1.0 / (1.0 + jnp.exp(-g))) * u).astype(BF))
+        p = jnp.concatenate(ps, 1)
+        for n in range(0, D, 256):
+            acc[rows, n:n + 256] += dot(p, WD[slot, :, n:n + 256])
+
+    def bwd_ab(slot, t, saved):
+        rows = pl.ds(t * TB, TB)
+        a = None if saved else ab[rows, :]
         dy = dyb[rows, :]
         for n in range(0, FC, 256):
-            g = dot(a, WG[slot, :, n:n + 256])
-            u = dot(a, WU[slot, :, n:n + 256])
             dp = dot_t(dy, WD[slot, n:n + 256, :]).astype(BF).astype(F32)
+            if saved:
+                g, u = gst[t % 2, :, n:n + 256], ust[t % 2, :, n:n + 256]
+            else:
+                g = dot(a, WG[slot, :, n:n + 256])
+                u = dot(a, WU[slot, :, n:n + 256])
             sig = 1.0 / (1.0 + jnp.exp(-g))
             silu = g * sig
             p = (silu * u).astype(BF)
             pT[n:n + 256, rows] = p.T
             dub[rows, n:n + 256] = (dp * silu).astype(BF)
             dgb[rows, n:n + 256] = (dp * u * (sig * (1.0 + g * (1.0 - sig)))).astype(BF)
-        acc[rows, :] += dot_t(dgb[rows, :], WG[slot]) + dot_t(dub[rows, :], WU[slot])
+
+    def bwd_c(slot, t):
+        for i in range(2):
+            rows = pl.ds(t * TB + i * TB // 2, TB // 2)
+            for n in range(0, D, 256):
+                acc[rows, n:n + 256] += dot_t(dgb[rows, :], WG[slot, n:n + 256, :]) + dot_t(dub[rows, :], WU[slot, n:n + 256, :])
 
     def norm_back(l):
         @pl.loop(0, T // 256)
@@ -283,71 +307,98 @@
         def _():
             send_ps(1)
 
-        @pl.loop(0, NB)
-        def _(t):
-            fwd_block(j % 2, t)
-
-            @pl.when(t == 0)
-            def _():
+        for t in range(NB):
+            if t >= 2:
+                for copy in gu_copies(j, t - 2, True):
+                    copy.wait()
+            else:
+                @pl.when(j > 0)
+                def _():
+                    for copy in gu_copies(j - 1, t + NB - 2, True):
+                        copy.wait()
+            fwd_block(j % 2, j, t)
+            for copy in gu_copies(j, t, True):
+                copy.start()
+            if t == 0:
                 stage1(j + 2)
-
-            @pl.when(t == 1)
-            def _():
+            if t == 1:
                 stage2(j + 1)
-
-            @pl.when(t == 2)
-            def _():
+            if t == 2:
                 ready(j + 1)
                 load(j + 1)
+
+    for t in (NB - 2, NB - 1):
+        for copy in gu_copies(NC - 1, t, True):
+            copy.wait()
 
     @pl.loop(0, T // 256)
     def _(t):
         rows = pl.ds(m_of(t * 256, 256), 256)
         hb[1, rows, :] = (hb[0, rows, :].astype(F32) + acc[rows, :].astype(BF).astype(F32)).astype(BF)
 
-    @pl.loop(0, 2)
-    def _(phase):
+    for phase in range(2):
         norm(1 - phase, True)
+        if phase == 1:
+            for t in range(2):
+                for copy in gu_copies(0, t, False):
+                    copy.start()
 
         @pl.loop(0, NC)
         def _(j):
             s = phase * NC + j
             step = NC + s
+            slot = step % 2
             loaded(step)
 
-            @pl.loop(0, NB)
-            def _(t):
-                bwd_block(step % 2, t)
-
-                @pl.when(t == 0)
-                def _():
-                    @pl.when(s >= 1)
-                    def _():
-                        reduce_x(s - 1)
-
-                    @pl.when(step + 2 < 2 * NC)
-                    def _():
-                        stage1(step + 2)
-
-                @pl.when(t == 1)
-                def _():
-                    @pl.when(step + 1 < 2 * NC)
-                    def _():
-                        stage2(step + 1)
-
-                @pl.when(t == 2)
-                def _():
-                    @pl.when(s >= 2)
-                    def _():
-                        finish(s - 2)
-
-                    @pl.when(step + 1 < 2 * NC)
-                    def _():
-                        ready(step + 1)
-
-                    @pl.when(step + 1 < 3 * NC)
-                    def _():
-                        load(step + 1)
+            def ab_of(t):
+                if phase == 1:
+                    for copy in gu_copies(j, t, False):
+                        copy.wait()
+                bwd_ab(slot, t, phase == 1)
+                if phase == 1:
+                    if t + 2 < NB:
+                        for copy in gu_copies(j, t + 2, False):
+                            copy.start()
+                    else:
+                        @pl.when(j + 1 < NC)
+                        def _():
+                            for copy in gu_copies(j + 1, t + 2 - NB, False):
+                                copy.start()
+
+            ab_of(0)
+
+            @pl.when(s >= 1)
+            def _():
+                reduce_x(s - 1)
+
+            @pl.when(step + 2 < 2 * NC)
+            def _():
+                stage1(step + 2)
+
+            bwd_c(slot, 0)
+            ab_of(1)
+            bwd_c(slot, 1)
+            ab_of(2)
+
+            @pl.when(step + 1 < 2 * NC)
+            def _():
+                stage2(step + 1)
+
+            @pl.when(s >= 2)
+            def _():
+                finish(s - 2)
+
+            @pl.when(step + 1 < 2 * NC)
+            def _():
+                ready(step + 1)
+
+            @pl.when(step + 1 < 3 * NC)
+            def _():
+                load(step + 1)
+
+            bwd_c(slot, 2)
+            ab_of(3)
+            bwd_c(slot, 3)
             produce(s)
         norm_back(1 - phase)
 
@@ -380,9 +431,11 @@
         outs = [sds((T, D), BF), sds(wg.shape, BF), sds(wu.shape, BF), sds(wd.shape, BF)]
         outs += [sds(s, BF) for s in (gate, gate, down) * 2]
         outs += [sds(t.shape, BF) for t in (wg, wu, wd)]
+        outs += [sds((NC, T, FC), F32)] * 2
         scratch = [V((2, T, D), BF), V((T, D), BF), V((T, D), BF), V((D, T), BF), V((T, D), F32),
                    V((2, D, FC), BF), V((2, D, FC), BF), V((2, FC, D), BF),
-                   V((FC, T), BF), V((T, FC), BF), V((T, FC), BF)]
+                   V((FC, T), BF), V((T, FC), BF), V((T, FC), BF),
+                   V((2, TB, FC), F32), V((2, TB, FC), F32), DMA((2, 2))]
         h3 = ((2 * Q, FC), (2 * Q, FC), (2 * S, D))
         q3 = ((Q, FC), (Q, FC), (S, D))
         scratch += [V(s, BF) for s in h3] + [V((2, *s), BF) for s in h3] + [V((2, *s), F32) for s in h3]

time: 314 us -> 283 us (0.901)
  Pallas kernels: 303 us -> 272 us
    pallas_call x1, Pallas kernels: 303 us -> 272 us  [local(): pl.pallas_call(functools.partial(kernel, NC), out_shape=outs, in_specs=[h...]
where the time goes in v2:
time: 283 us
  Pallas kernels  272 us (96%)
  local copies, waits for them, and re-layouts  10.3 us (4%)
    pallas_call x1, Pallas kernels, local(): pl.pallas_call(functools.partial(kernel, NC), out_shape=outs, in_specs=[h...  272 us
    unnamed x10, local copies, waits for them, and re-layouts  10.3 us

profile of v2, /device:TPU:0, one launch (start us, length us, event | category | flops | bytes accessed | tf_op | source)
XLA Modules:
  0.0 282.6 jit_solution(18148628599497851086)
XLA Ops:
  0.6 271.6 %shard_map.84 = (bf16[2048,768]{1,0:T(8,128)(2,1)}, bf16[2,192,3072]{2,1,0:T(8,128)(2,1)}, bf16[2,192,3072]{2,1,0:T(8,128)(2,1)}, bf16[2,768,768]{2,1,0:T(8,128)...) custom-call(bf16[2048,768]{1,0:T(8,128)(2,1)} %bitcast.4, ...), custom_call_target="tpu_custom_call" | custom-call | tf_op jit(solution)/shard_map/pallas_call | solution.py:446
  272.3 0.0 copy-start.2
  272.3 3.9 %copy.13 = bf16[1,2048,768]{2,1,0:T(8,128)(2,1)} copy(bf16[1,2048,768]{2,1,0:T(8,128)(2,1)} %bitcast.3) | data formatting | bytes 6291456
  276.2 0.0 copy-done.2
  276.2 0.0 copy-start.1
  276.2 1.4 copy.14
  277.6 1.1 copy-done.1
  278.7 0.0 copy-start
  278.7 1.4 copy.15
  280.1 1.1 copy-done
  281.2 1.4 copy.16
Async XLA Ops:
  272.3 3.9 %copy-start.2 = (bf16[2,192,3072]{2,1,0:T(8,128)(2,1)S(1)}, bf16[2,192,3072]{2,1,0:T(8,128)(2,1)}, u32[]{:S(2)}) copy-start(bf16[2,192,3072]{2,1,0:T(8,128)(2,1)} %get-tuple-element.17) | copy-start | bytes 7077892
  276.2 2.5 copy-start.1
  278.7 2.5 copy-start

commit v3 on v2

--- a/solution.py
+++ b/solution.py
@@ -151,36 +151,41 @@
     def to_x(m, s):
         return remote(SX[m].at[s % 2], RX[m].at[s % 4], x_s.at[m, s % 2], x_r.at[m, s % 4], xp)
 
-    def grads(m, part, n):
+    def grads(m, part, n, l=0):
         rows = pl.ds(m_of(part * HR[m], HR[m]), HR[m])
         if m == 2:
             return dot(pT[rows, :], dyb[:, n:n + 256])
-        return dot(aT[rows, :], (dgb, dub)[m][:, n:n + 256])
-
-    def produce(s):
-        slot = s % 2
+        return dot(aT[l, rows, :], (dgb, dub)[m][:, n:n + 256])
+
+    def grads_first(slot, l):
         for n in range(0, D, 256):
             szd[:, n:n + 256] = grads(2, 1 - k, n).astype(BF)
             Gd[slot, :, n:n + 256] = grads(2, k, n)
         for m in (0, 1):
             for n in range(0, FC, 256):
-                SZ[m][:, n:n + 256] = grads(m, 1 - k, n).astype(BF)
-        for m in (2, 0, 1):
-            to_z(m, s).start()
+                SZ[m][:, n:n + 256] = grads(m, 1 - k, n, l).astype(BF)
+
+    def grads_mine(slot, l):
         for m in (0, 1):
             for n in range(0, FC, 256):
-                G32[m][slot, :, n:n + 256] = grads(m, k, n)
-
-    def reduce_x(s):
-        for m in (2, 0, 1):
+                G32[m][slot, :, n:n + 256] = grads(m, k, n, l)
+
+    def chip_wait(ms, s):
+        for m in ms:
             @pl.when(s >= 2)
             def _():
                 to_x(m, s).wait_send()
             to_z(m, s).wait()
+
+    def chip_sum(ms, slot):
+        for m in ms:
             mine, other = pl.ds(m_of(c * QR[m], QR[m]), QR[m]), pl.ds(m_of((1 - c) * QR[m], QR[m]), QR[m])
-            SX[m][s % 2] = (G32[m][s % 2, other] + RZ[m][s % 2, other].astype(F32)).astype(BF)
+            SX[m][slot] = (G32[m][slot, other] + RZ[m][slot, other].astype(F32)).astype(BF)
+            G32[m][slot, mine] += RZ[m][slot, mine].astype(F32)
+
+    def chip_send(ms, s):
+        for m in ms:
             to_x(m, s).start()
-            G32[m][s % 2, mine] += RZ[m][s % 2, mine].astype(F32)
 
     def out_copies(s):
         l, j = 1 - s // NC, s % NC
@@ -193,38 +198,51 @@
         for m in range(3):
             pltpu.make_async_copy(OB[m].at[s % 2], OB[m].at[s % 2], o_s.at[m, s % 2]).wait()
 
-    def finish(s):
+    def last_wait(s):
         @pl.when(s >= 2)
         def _():
             out_wait(s)
-        for m in (2, 0, 1):
+        for m in range(3):
             to_x(m, s).wait_recv()
+
+    def last_sum(slot, rx):
+        for m in range(3):
             mine = pl.ds(m_of(c * QR[m], QR[m]), QR[m])
-            OB[m][s % 2] = (G32[m][s % 2, mine] + RX[m][s % 4].astype(F32)).astype(BF)
+            OB[m][slot] = (G32[m][slot, mine] + RX[m][rx].astype(F32)).astype(BF)
+
+    def last_out(s):
         for copy in out_copies(s):
             copy.start()
 
+    def finish(s):
+        last_wait(s)
+        last_sum(s % 2, s % 4)
+        last_out(s)
+
     def scale_of(wide):
         return lax.rsqrt(jnp.mean(wide * wide, -1, keepdims=True) + 1e-6)
 
-    def norm(l, transposed):
+    def norm(l):
         @pl.loop(0, T // 256)
         def _(t):
             rows = pl.ds(m_of(t * 256, 256), 256)
-            wide = hb[l, rows, :].astype(F32)
+            wide = hb[0, rows, :].astype(F32)
+            if l:
+                h = (wide + acc[rows, :].astype(BF).astype(F32)).astype(BF)
+                hb[1, rows, :] = h
+                wide = h.astype(F32)
             a = (wide * scale_of(wide)).astype(BF)
             ab[rows, :] = a
             acc[rows, :] = jnp.zeros((256, D), F32)
-            if transposed:
-                at = a.T
-                for q in range(4):
-                    aT[pl.ds(pos(q) * Q, Q), rows] = at[q * Q:(q + 1) * Q]
+            at = a.T
+            for q in range(4):
+                aT[l, pl.ds(pos(q) * Q, Q), rows] = at[q * Q:(q + 1) * Q]
 
     def gu_copies(j, t, out):
         rows = pl.ds(m_of(t * TB, TB), TB)
         for i, (v, h) in enumerate(((gst, g_h), (ust, u_h))):
-            pair = (v.at[t % 2], h.at[j, rows, :])
-            yield pltpu.make_async_copy(*(pair if out else pair[::-1]), gu_s.at[i, t % 2])
+            pair = (v.at[t], h.at[j, rows, :])
+            yield pltpu.make_async_copy(*(pair if out else pair[::-1]), gu_s.at[i, t])
 
     def fwd_block(slot, j, t):
         rows = pl.ds(t * TB, TB)
@@ -233,8 +251,8 @@
         for n in range(0, FC, 256):
             g = dot(a, WG[slot, :, n:n + 256])
             u = dot(a, WU[slot, :, n:n + 256])
-            gst[t % 2, :, n:n + 256] = g
-            ust[t % 2, :, n:n + 256] = u
+            gst[t, :, n:n + 256] = g
+            ust[t, :, n:n + 256] = u
             ps.append((g * (1.0 / (1.0 + jnp.exp(-g))) * u).astype(BF))
         p = jnp.concatenate(ps, 1)
         for n in range(0, D, 256):
@@ -247,7 +265,7 @@
         for n in range(0, FC, 256):
             dp = dot_t(dy, WD[slot, n:n + 256, :]).astype(BF).astype(F32)
             if saved:
-                g, u = gst[t % 2, :, n:n + 256], ust[t % 2, :, n:n + 256]
+                g, u = gst[t, :, n:n + 256], ust[t, :, n:n + 256]
             else:
                 g = dot(a, WG[slot, :, n:n + 256])
                 u = dot(a, WU[slot, :, n:n + 256])
@@ -273,6 +291,7 @@
             da = acc[rows, :].astype(BF).astype(F32)
             inner = jnp.sum(da * wide, -1, keepdims=True)
             dh = da * sc - wide * (sc * sc * sc * inner * (1.0 / D))
+            acc[rows, :] = jnp.zeros((256, D), F32)
             dyb[rows, :] = (dyb[rows, :].astype(F32) + dh.astype(BF).astype(F32)).astype(BF)
 
     in_x = pltpu.make_async_copy(x_h, hb.at[0], io_s.at[0])
@@ -290,7 +309,7 @@
     def _(s):
         send_x(s)
     in_x.wait()
-    norm(0, False)
+    norm(0)
     in_dy.wait()
     stage1(0)
     stage1(1)
@@ -308,14 +327,10 @@
             send_ps(1)
 
         for t in range(NB):
-            if t >= 2:
-                for copy in gu_copies(j, t - 2, True):
+            @pl.when(j > 0)
+            def _():
+                for copy in gu_copies(j - 1, t, True):
                     copy.wait()
-            else:
-                @pl.when(j > 0)
-                def _():
-                    for copy in gu_copies(j - 1, t + NB - 2, True):
-                        copy.wait()
             fwd_block(j % 2, j, t)
             for copy in gu_copies(j, t, True):
                 copy.start()
@@ -327,21 +342,21 @@
                 ready(j + 1)
                 load(j + 1)
 
-    for t in (NB - 2, NB - 1):
+    for t in range(NB):
         for copy in gu_copies(NC - 1, t, True):
             copy.wait()
 
-    @pl.loop(0, T // 256)
-    def _(t):
-        rows = pl.ds(m_of(t * 256, 256), 256)
-        hb[1, rows, :] = (hb[0, rows, :].astype(F32) + acc[rows, :].astype(BF).astype(F32)).astype(BF)
+    stage2(NC + 1)
+    norm(1)
 
     for phase in range(2):
-        norm(1 - phase, True)
         if phase == 1:
-            for t in range(2):
+            for t in range(NB):
                 for copy in gu_copies(0, t, False):
                     copy.start()
+
+        def when(yes):
+            return lambda f: pl.when(yes)(f) if phase == 0 else f()
 
         @pl.loop(0, NC)
         def _(j):
@@ -349,71 +364,95 @@
             step = NC + s
             slot = step % 2
             loaded(step)
-
-            def ab_of(t):
-                if phase == 1:
+            if phase == 1:
+                for t in range(NB):
                     for copy in gu_copies(j, t, False):
                         copy.wait()
-                bwd_ab(slot, t, phase == 1)
-                if phase == 1:
-                    if t + 2 < NB:
-                        for copy in gu_copies(j, t + 2, False):
-                            copy.start()
-                    else:
-                        @pl.when(j + 1 < NC)
-                        def _():
-                            for copy in gu_copies(j + 1, t + 2 - NB, False):
-                                copy.start()
-
-            ab_of(0)
-
-            @pl.when(s >= 1)
+            bwd_ab(slot, 0, phase == 1)
+
+            @when(s >= 1)
             def _():
-                reduce_x(s - 1)
-
-            @pl.when(step + 2 < 2 * NC)
-            def _():
-                stage1(step + 2)
-
-            bwd_c(slot, 0)
-            ab_of(1)
-            bwd_c(slot, 1)
-            ab_of(2)
-
-            @pl.when(step + 1 < 2 * NC)
-            def _():
-                stage2(step + 1)
-
-            @pl.when(s >= 2)
-            def _():
-                finish(s - 2)
-
-            @pl.when(step + 1 < 2 * NC)
-            def _():
-                ready(step + 1)
+                chip_wait(range(3), s - 1)
+                chip_sum(range(3), (s + 1) % 2)
+                chip_send(range(3), s - 1)
+
+            if phase == 0:
+                @pl.when(step + 2 < 2 * NC)
+                def _():
+                    stage1(step + 2)
+
+                @pl.when(step + 1 < 2 * NC)
+                def _():
+                    ready(step + 1)
 
             @pl.when(step + 1 < 3 * NC)
             def _():
                 load(step + 1)
 
-            bwd_c(slot, 2)
-            ab_of(3)
-            bwd_c(slot, 3)
-            produce(s)
-        norm_back(1 - phase)
+            bwd_c(slot, 0)
+            for t in range(1, NB):
+                bwd_ab(slot, t, phase == 1)
+                bwd_c(slot, t)
+
+            @when(s >= 2)
+            def _():
+                last_wait(s - 2)
+
+            if phase == 1:
+                @pl.when(j + 1 < NC)
+                def _():
+                    for t in range(NB):
+                        for copy in gu_copies(j + 1, t, False):
+                            copy.start()
+
+            last_sum(s % 2, (s + 2) % 4)
+            grads_first(s % 2, 1 - phase)
+            for m in (2, 0, 1):
+                to_z(m, s).start()
+
+            @when(s >= 2)
+            def _():
+                last_out(s - 2)
+
+            grads_mine(s % 2, 1 - phase)
+
+            if phase == 0:
+                @pl.when(step + 2 < 2 * NC)
+                def _():
+                    stage2(step + 2)
+        if phase == 0:
+            norm_back(1)
 
     last = 2 * NC - 1
+    chip_wait(range(3), last)
+    chip_sum(range(3), last % 2)
+    chip_send(range(3), last)
+    norm_back(0)
     out_dx = pltpu.make_async_copy(dyb, dx_o, io_s.at[0])
     out_dx.start()
-    reduce_x(last)
+    drain_ag()
     finish(last - 1)
-    drain_ag()
     finish(last)
     for s in (last - 1, last):
         for m in range(3):
             to_x(m, s).wait_send()
         out_wait(s)
     out_dx.wait()
+
+
+def copy_kernel(*refs):
+    n = (len(refs) - 2) // 3
+    src, dst, held, s_in, s_out = refs[:n], refs[n:2 * n], refs[2 * n:3 * n], refs[-2], refs[-1]
+    pieces = [(i, pl.ds(p * (src[i].shape[0] // 4), src[i].shape[0] // 4)) for i in range(n) for p in range(4)]
+    ins = [pltpu.make_async_copy(src[i].at[r], held[i].at[r], s_in.at[x]) for x, (i, r) in enumerate(pieces)]
+    outs = [pltpu.make_async_copy(held[i].at[r], dst[i].at[r], s_out.at[x]) for x, (i, r) in enumerate(pieces)]
+    for copy in ins:
+        copy.start()
+    for x in range(len(pieces)):
+        ins[x].wait()
+        outs[x].start()
+    for copy in outs:
+        copy.wait()
 
 
 def solution(mesh):
@@ -432,10 +471,10 @@
         outs += [sds(s, BF) for s in (gate, gate, down) * 2]
         outs += [sds(t.shape, BF) for t in (wg, wu, wd)]
         outs += [sds((NC, T, FC), F32)] * 2
-        scratch = [V((2, T, D), BF), V((T, D), BF), V((T, D), BF), V((D, T), BF), V((T, D), F32),
+        scratch = [V((2, T, D), BF), V((T, D), BF), V((T, D), BF), V((2, D, T), BF), V((T, D), F32),
                    V((2, D, FC), BF), V((2, D, FC), BF), V((2, FC, D), BF),
                    V((FC, T), BF), V((T, FC), BF), V((T, FC), BF),
-                   V((2, TB, FC), F32), V((2, TB, FC), F32), DMA((2, 2))]
+                   V((T // TB, TB, FC), F32), V((T // TB, TB, FC), F32), DMA((2, T // TB))]
         h3 = ((2 * Q, FC), (2 * Q, FC), (2 * S, D))
         q3 = ((Q, FC), (Q, FC), (S, D))
         scratch += [V(s, BF) for s in h3] + [V((2, *s), BF) for s in h3] + [V((2, *s), F32) for s in h3]
@@ -451,7 +490,16 @@
             scratch_shapes=scratch,
             compiler_params=pltpu.CompilerParams(collective_id=0, has_side_effects=True, vmem_limit_bytes=67043328),
         )(x[0], dy[0], wg, wu, wd)
-        return (res[0][None], *res[1:4])
+        grads = [t.reshape(-1, t.shape[-1]) for t in res[:4]]
+        n = len(grads)
+        dx, *dw = pl.pallas_call(
+            copy_kernel,
+            out_shape=[sds(t.shape, BF) for t in grads],
+            in_specs=[hbm] * n,
+            out_specs=[hbm] * n,
+            scratch_shapes=[V(t.shape, BF) for t in grads] + [DMA((4 * n,)), DMA((4 * n,))],
+        )(*grads)
+        return (dx[None], *(t.reshape(w.shape) for t, w in zip(dw, (wg, wu, wd))))
 
     seq, w = P(("rep", "dp"), None, None), P(None, "dp", None)
     grad = P("rep", "dp", None)

time: 283 us -> 272 us (0.961)
  local copies, waits for them, and re-layouts: 10.3 us -> 0 us
    unnamed x10 -> x0, local copies, waits for them, and re-layouts: 10.3 us -> none
    pallas_call x1, Pallas kernels: 272 us -> 263 us  [local(): pl.pallas_call(functools.partial(kernel, NC), out_shape=outs, in_specs=[h...]
    pallas_call x0 -> x1, Pallas kernels: none -> 7.95 us  [local(): pl.pallas_call(copy_kernel, out_shape=[sds(t.shape, BF) for t in grads],...]
where the time goes in v3:
time: 272 us
  Pallas kernels  271 us (100%)
    pallas_call x1, Pallas kernels, local(): pl.pallas_call(functools.partial(kernel, NC), out_shape=outs, in_specs=[h...  263 us
    pallas_call x1, Pallas kernels, local(): pl.pallas_call(copy_kernel, out_shape=[sds(t.shape, BF) for t in grads],...  7.95 us

profile of v3, /device:TPU:0, one launch (start us, length us, event | category | flops | bytes accessed | tf_op | source)
XLA Modules:
  0.0 272.0 jit_solution(16540708426074899095)
XLA Ops:
  0.6 263.3 %shard_map.84 = (bf16[2048,768]{1,0:T(8,128)(2,1)}, bf16[2,192,3072]{2,1,0:T(8,128)(2,1)}, bf16[2,192,3072]{2,1,0:T(8,128)(2,1)}, bf16[2,768,768]{2,1,0:T(8,128)...) custom-call(bf16[2048,768]{1,0:T(8,128)(2,1)} %bitcast.9, ...), custom_call_target="tpu_custom_call" | custom-call | tf_op jit(solution)/shard_map/pallas_call | solution.py:485
  263.9 8.0 %shard_map.85 = (bf16[2048,768]{1,0:T(8,128)(2,1)}, bf16[384,3072]{1,0:T(8,128)(2,1)}, bf16[384,3072]{1,0:T(8,128)(2,1)}, bf16[1536,768]{1,0:T(8,128)(2,1)}) custom-call(bf16[2048,768]{1,0:T(8,128)(2,1)} %get-tuple-element.12.refs_0_, bf16[384,3072]{1,0:T(8,128)(2,1)} %bitcast.11, bf16[384,3072]{1,0:T(8,128)(2,1)} %bitcast.12, bf16[1536,768]{1,0:T(8,128)(2,1)} %bitcast.13), custom_call_target="tpu_custom_call" | custom-call | tf_op jit(solution)/shard_map/pallas_call | solution.py:495

commit v4 on v3

--- a/solution.py
+++ b/solution.py
@@ -369,6 +369,8 @@
                     for copy in gu_copies(j, t, False):
                         copy.wait()
             bwd_ab(slot, 0, phase == 1)
+            bwd_c(slot, 0)
+            bwd_ab(slot, 1, phase == 1)
 
             @when(s >= 1)
             def _():
@@ -389,8 +391,8 @@
             def _():
                 load(step + 1)
 
-            bwd_c(slot, 0)
-            for t in range(1, NB):
+            bwd_c(slot, 1)
+            for t in range(2, NB):
                 bwd_ab(slot, t, phase == 1)
                 bwd_c(slot, t)
 

time: 272 us -> 273 us (level)
  no operation moved by 1% of the time
where the time goes in v4:
time: 273 us
  Pallas kernels  272 us (100%)
    pallas_call x1, Pallas kernels, local(): pl.pallas_call(functools.partial(kernel, NC), out_shape=outs, in_specs=[h...  264 us
    pallas_call x1, Pallas kernels, local(): pl.pallas_call(copy_kernel, out_shape=[sds(t.shape, BF) for t in grads],...  7.95 us

profile of v4, /device:TPU:0, one launch (start us, length us, event | category | flops | bytes accessed | tf_op | source)
XLA Modules:
  0.0 272.7 jit_solution(3965476830865189306)
XLA Ops:
  0.6 263.9 %shard_map.84 = (bf16[2048,768]{1,0:T(8,128)(2,1)}, bf16[2,192,3072]{2,1,0:T(8,128)(2,1)}, bf16[2,192,3072]{2,1,0:T(8,128)(2,1)}, bf16[2,768,768]{2,1,0:T(8,128)...) custom-call(bf16[2048,768]{1,0:T(8,128)(2,1)} %bitcast.9, ...), custom_call_target="tpu_custom_call" | custom-call | tf_op jit(solution)/shard_map/pallas_call | solution.py:487
  264.6 8.0 %shard_map.85 = (bf16[2048,768]{1,0:T(8,128)(2,1)}, bf16[384,3072]{1,0:T(8,128)(2,1)}, bf16[384,3072]{1,0:T(8,128)(2,1)}, bf16[1536,768]{1,0:T(8,128)(2,1)}) custom-call(bf16[2048,768]{1,0:T(8,128)(2,1)} %get-tuple-element.12.refs_0_, bf16[384,3072]{1,0:T(8,128)(2,1)} %bitcast.11, bf16[384,3072]{1,0:T(8,128)(2,1)} %bitcast.12, bf16[1536,768]{1,0:T(8,128)(2,1)} %bitcast.13), custom_call_target="tpu_custom_call" | custom-call | tf_op jit(solution)/shard_map/pallas_call | solution.py:497

commit v5 on v3

--- a/solution.py
+++ b/solution.py
@@ -326,17 +326,21 @@
         def _():
             send_ps(1)
 
-        for t in range(NB):
+        for ts in ((0, 1), (2,), (3,)):
+            t = ts[-1]
+
             @pl.when(j > 0)
             def _():
-                for copy in gu_copies(j - 1, t, True):
-                    copy.wait()
-            fwd_block(j % 2, j, t)
-            for copy in gu_copies(j, t, True):
-                copy.start()
-            if t == 0:
+                for i in ts:
+                    for copy in gu_copies(j - 1, i, True):
+                        copy.wait()
+            for i in ts:
+                fwd_block(j % 2, j, i)
+            for i in ts:
+                for copy in gu_copies(j, i, True):
+                    copy.start()
+            if t == 1:
                 stage1(j + 2)
-            if t == 1:
                 stage2(j + 1)
             if t == 2:
                 ready(j + 1)

time: 272 us -> 274 us (level)
  no operation moved by 1% of the time
where the time goes in v5:
time: 274 us
  Pallas kernels  273 us (100%)
    pallas_call x1, Pallas kernels, local(): pl.pallas_call(functools.partial(kernel, NC), out_shape=outs, in_specs=[h...  265 us
    pallas_call x1, Pallas kernels, local(): pl.pallas_call(copy_kernel, out_shape=[sds(t.shape, BF) for t in grads],...  7.95 us

profile of v5, /device:TPU:0, one launch (start us, length us, event | category | flops | bytes accessed | tf_op | source)
XLA Modules:
  0.0 274.0 jit_solution(15216049741923394071)
XLA Ops:
  0.6 265.2 %shard_map.84 = (bf16[2048,768]{1,0:T(8,128)(2,1)}, bf16[2,192,3072]{2,1,0:T(8,128)(2,1)}, bf16[2,192,3072]{2,1,0:T(8,128)(2,1)}, bf16[2,768,768]{2,1,0:T(8,128)...) custom-call(bf16[2048,768]{1,0:T(8,128)(2,1)} %bitcast.9, ...), custom_call_target="tpu_custom_call" | custom-call | tf_op jit(solution)/shard_map/pallas_call | solution.py:489
  265.8 8.0 %shard_map.85 = (bf16[2048,768]{1,0:T(8,128)(2,1)}, bf16[384,3072]{1,0:T(8,128)(2,1)}, bf16[384,3072]{1,0:T(8,128)(2,1)}, bf16[1536,768]{1,0:T(8,128)(2,1)}) custom-call(bf16[2048,768]{1,0:T(8,128)(2,1)} %get-tuple-element.12.refs_0_, bf16[384,3072]{1,0:T(8,128)(2,1)} %bitcast.11, bf16[384,3072]{1,0:T(8,128)(2,1)} %bitcast.12, bf16[1536,768]{1,0:T(8,128)(2,1)} %bitcast.13), custom_call_target="tpu_custom_call" | custom-call | tf_op jit(solution)/shard_map/pallas_call | solution.py:499
